TPU v7x, 256 devices: a whole 4x4x8 slice. The times are simulated.
256 devices in a mesh: band: 64 (over y, z, core), feat: 4 (over x).
Axes of the slice: x: 4, y: 4, z: 8, core: 2. Of those that a mesh axis runs over, the one named last changes fastest.
Arguments:
- grid_latent: bfloat16 [131072, 512], P('band', 'feat'), may hold values from -6 to 6
- mesh_latent: bfloat16 [10240, 512], P('band', 'feat'), may hold values from -6 to 6
- edge_latent: bfloat16 [64, 4, 2048, 512], P('band', 'feat'), may hold values from -6 to 6
- edge_src: int32 [64, 8192], P('band'), may hold values from 0 to 2047
- edge_dst: int32 [64, 4, 2048], P('band', 'feat'), may hold values from 0 to 160, as said below
- edge_w1: bfloat16 [1536, 512], replicated, may hold values from -0.15625 to 0.15625
- edge_b1: float32 [512], replicated, may hold values from -3 to 3
- edge_w2: bfloat16 [512, 512], replicated, may hold values from -0.25 to 0.25
- edge_b2: float32 [512], replicated, may hold values from -2 to 2
- edge_gain: float32 [512], replicated, may hold values from 0.25 to 1.75
- edge_shift: float32 [512], replicated, may hold values from -2 to 2
- node_w1: bfloat16 [1024, 512], replicated, may hold values from -0.1875 to 0.1875
- node_b1: float32 [512], replicated, may hold values from -3 to 3
- node_w2: bfloat16 [512, 512], replicated, may hold values from -0.25 to 0.25
- node_b2: float32 [512], replicated, may hold values from -2 to 2
- node_gain: float32 [512], replicated, may hold values from 0.25 to 1.75
- node_shift: float32 [512], replicated, may hold values from -2 to 2
Outputs:
- mesh_new: bfloat16 [10240, 512], P('band', 'feat')
Inputs may be any that keep to these rules, and one draw needn't show every extreme that they name: `edge_src`: entry [s, d * 128 + j] is the grid row, counted within band index s, that sends slot j of the edges from band index s to band index d; empty slots hold some row too. `edge_dst`: entry [d, f, s * 32 + q] is the mesh node, counted within band index d, that receives slot f * 32 + q of the edges from band index s to band index d, or 160 where that slot is empty. The used slots of a pair come first; a pair has at most 128 used slots. Each receiving band index d hears only from the sending band indices of one latitude span of consecutive indices (edges are local), which lies anywhere along band since mesh partitions are face-major; other pairs are empty. In every draw some band indices receive 128 from every band index of their span.
All inputs are finite; a program needn't handle non-finite values.
Results may differ from a plain program's by a relative error of at most 0.011.
Values may be sent and summed in bfloat16 or wider, within the bound.
No kernel may reach another device: no remote copies, remote signals or barrier semaphores. Data moves between devices by JAX's collectives and lax.ppermute only.
A program may use at most 64 MiB of HBM per device.

v0:
```python
import math
import jax
import jax.numpy as jnp
from jax import lax
from jax.sharding import PartitionSpec as P

EPSILON = 1e-05


def cut_along(value, dim, length):
    shape = value.shape
    tiles = value.reshape(*shape[:dim], length, shape[dim] // length, *shape[dim + 1 :])
    return jnp.moveaxis(tiles, dim, 0)


def laid_out(tiles, dim):
    tiles = jnp.moveaxis(tiles, 0, dim)
    shape = tiles.shape
    return tiles.reshape(*shape[:dim], shape[dim] * shape[dim + 1], *shape[dim + 2 :])


def joined_exchange(value, axis, axes, splits, concats):
    sizes = [lax.axis_size(a) for a in axes]
    tiles = cut_along(value, splits[0], sizes[0])
    tiles = jnp.moveaxis(cut_along(tiles, splits[1] + 1, sizes[1]), 0, 1)
    inside = tiles.shape[2:]
    tiles = tiles.reshape(-1, *inside)
    tiles = lax.all_to_all(tiles, axis, split_axis=0, concat_axis=0, tiled=True)
    tiles = laid_out(tiles.reshape(*sizes, *inside), concats[0] + 1)
    return laid_out(tiles, concats[1])


def from_everyone(value, axis):
    length = lax.axis_size(axis)
    return lax.all_to_all(
        jnp.broadcast_to(value[None], (length, *value.shape)), axis, 0, 0, tiled=True
    )


def taken_together(value, axis):
    everything = from_everyone(value, axis)
    return jnp.sum(everything.astype(jnp.float32), axis=0)


def normalize(values, norm_gain, norm_shift):
    average = jnp.mean(values, -1, keepdims=True)
    centered = values - average
    variance = jnp.mean(centered * centered, -1, keepdims=True)
    return centered * lax.rsqrt(variance + EPSILON) * norm_gain + norm_shift


def node_step(row_block, summed, node_w1, node_b1, node_w2, node_b2, node_gain, node_shift):
    full_width = row_block.shape[1]
    hidden = jnp.dot(row_block, node_w1[:full_width], preferred_element_type=jnp.float32)
    hidden = (
        hidden
        + jnp.dot(
            summed.astype(jnp.bfloat16), node_w1[full_width:], preferred_element_type=jnp.float32
        )
        + node_b1
    )
    active = jax.nn.silu(hidden).astype(jnp.bfloat16)
    update = jnp.dot(active, node_w2, preferred_element_type=jnp.float32) + node_b2
    return (row_block.astype(jnp.float32) + normalize(update, node_gain, node_shift)).astype(
        jnp.bfloat16
    )


def select_rows(table, indices):
    total = indices.shape[0]
    block_rows = math.gcd(total, 512)
    grouped = indices.reshape(total // block_rows, block_rows)

    def one_block(block_ids):
        row_ids = lax.broadcasted_iota(jnp.int32, (block_rows, table.shape[0]), 1)
        onehot = (row_ids == block_ids[:, None]).astype(table.dtype)
        return jnp.dot(onehot, table, preferred_element_type=jnp.float32).astype(table.dtype)

    return lax.map(one_block, grouped).reshape(total, table.shape[1])


def body(
    grid_latent,
    mesh_latent,
    edge_latent,
    edge_src,
    edge_dst,
    edge_w1,
    edge_b1,
    edge_w2,
    edge_b2,
    edge_gain,
    edge_shift,
    node_w1,
    node_b1,
    node_w2,
    node_b2,
    node_gain,
    node_shift,
):
    band_count = lax.axis_size("band")
    feat_count = lax.axis_size("feat")
    quarter = grid_latent.shape[1]
    full_width = quarter * feat_count
    mesh_count = mesh_latent.shape[0]
    picked = select_rows(grid_latent, edge_src.reshape(-1)).reshape(band_count, -1, quarter)
    arrived = joined_exchange(picked, ("band", "feat"), ("band", "feat"), (0, 1), (0, 2))
    senders = arrived.reshape(-1, full_width)
    own_edges = edge_latent.reshape(-1, full_width)
    targets = edge_dst.reshape(-1)
    recv_weight = edge_w1[2 * full_width :]
    portion = lax.all_gather(mesh_latent, "feat", axis=1, tiled=True)
    projected = jnp.dot(portion, recv_weight, preferred_element_type=jnp.float32)
    node_ids = lax.broadcasted_iota(jnp.int32, (mesh_count, targets.shape[0]), 0)
    clipped = jnp.minimum(targets, mesh_count - 1)
    pick_node = (node_ids == clipped[None, :]).astype(jnp.float32)
    receiver_part = lax.dot_general(
        pick_node,
        projected,
        (((0,), (0,)), ((), ())),
        precision=lax.Precision.HIGHEST,
        preferred_element_type=jnp.float32,
    )
    hidden = jnp.dot(own_edges, edge_w1[:full_width], preferred_element_type=jnp.float32)
    hidden = hidden + jnp.dot(
        senders, edge_w1[full_width : 2 * full_width], preferred_element_type=jnp.float32
    )
    hidden = hidden + receiver_part + edge_b1
    active = jax.nn.silu(hidden).astype(jnp.bfloat16)
    update = jnp.dot(active, edge_w2, preferred_element_type=jnp.float32) + edge_b2
    edge_new = (own_edges.astype(jnp.float32) + normalize(update, edge_gain, edge_shift)).astype(
        jnp.bfloat16
    )
    selector = (node_ids == targets[None, :]).astype(jnp.bfloat16)
    partial_sums = jnp.dot(selector, edge_new, preferred_element_type=jnp.float32)
    summed = taken_together(partial_sums.astype(jnp.bfloat16), "feat").astype(jnp.float32)
    updated = node_step(portion, summed, node_w1, node_b1, node_w2, node_b2, node_gain, node_shift)
    own_cols = lax.dynamic_slice_in_dim(updated, lax.axis_index("feat") * quarter, quarter, 1)
    return own_cols


def solution(mesh):
    placed = (
        P("band", "feat"),
        P("band", "feat"),
        P("band", "feat", None, None),
        P("band", None),
        P("band", "feat", None),
        P(),
        P(),
        P(),
        P(),
        P(),
        P(),
        P(),
        P(),
        P(),
        P(),
        P(),
        P(),
    )
    return jax.shard_map(
        body, mesh=mesh, in_specs=placed, out_specs=P("band", "feat"), check_vma=False
    )
```

profile of v0, /device:TPU:1, one launch (start us, length us, event | category | flops | bytes accessed | tf_op | source)
XLA Modules:
  0.0 142.4 jit_solution(16497475571590522492)
XLA Ops:
  0.5 1.5 %reduce.4 = s32[8192]{0:T(1024)S(1)} reduce(s32[1,8192]{1,0:T(1,128)} %param.22, s32[]{:T(128)} %broadcast.66), dimensions={0}, to_apply=%param.22.reduce_sub_computation.3 | reduce | bytes 65540 | tf_op args[3]
  2.0 40.9 %while.10 = (s32[]{:T(128)}, bf16[16,512,128]{2,1,0:T(8,128)(2,1)}, s32[16,512]{1,0:T(8,128)S(1)}, bf16[2048,128]{1,0:T(8,128)(2,1)}, s32[]{:T(128)}) while((s32[]{:T(128)}, bf16[16,512,128]{2,1,0:T(8,128)(2,1)}, s32[16,512]{1,0:T(8,128)S(1)}, bf16[2048,128]{1,0:T(8,128)(2,1)}, s32[]{:T(128)}) %tuple.21), condition=%wide.region_1.2_spmd, body=%wide.region_0.1_spmd.sunk | while | flops 269549568 | bytes 662081 | solution.py:79
  2.0 2.5 %fusion.47 = bf16[16,512,128]{2,1,0:T(8,128)(2,1)} fusion(bf16[16,512,128]{2,1,0:T(8,128)(2,1)} %get-tuple-element.73, s32[]{:T(128)} %get-tuple-element.72, bf16[2048,128]{1,0:T(8,128)(2,1)} %get-tuple-element.80, s32[512]{0:T(512)S(1)} %bitcast.42), kind=kOutput, calls=%fused_computation.5.clone.1 | convolution fusion | flops 269549568 | bytes 657920 | tf_op jit(solution)/shard_map/while/body/eval_jaxpr/dot_general | solution.py:77
  4.6 2.5 %fusion.47 = bf16[16,512,128]{2,1,0:T(8,128)(2,1)} fusion(bf16[16,512,128]{2,1,0:T(8,128)(2,1)} %get-tuple-element.73, s32[]{:T(128)} %get-tuple-element.72, bf16[2048,128]{1,0:T(8,128)(2,1)} %get-tuple-element.80, s32[512]{0:T(512)S(1)} %bitcast.42), kind=kOutput, calls=%fused_computation.5.clone.1 | convolution fusion | flops 269549568 | bytes 657920 | tf_op jit(solution)/shard_map/while/body/eval_jaxpr/dot_general | solution.py:77
  7.1 2.5 %fusion.47 = bf16[16,512,128]{2,1,0:T(8,128)(2,1)} fusion(bf16[16,512,128]{2,1,0:T(8,128)(2,1)} %get-tuple-element.73, s32[]{:T(128)} %get-tuple-element.72, bf16[2048,128]{1,0:T(8,128)(2,1)} %get-tuple-element.80, s32[512]{0:T(512)S(1)} %bitcast.42), kind=kOutput, calls=%fused_computation.5.clone.1 | convolution fusion | flops 269549568 | bytes 657920 | tf_op jit(solution)/shard_map/while/body/eval_jaxpr/dot_general | solution.py:77
  9.7 2.6 %fusion.47 = bf16[16,512,128]{2,1,0:T(8,128)(2,1)} fusion(bf16[16,512,128]{2,1,0:T(8,128)(2,1)} %get-tuple-element.73, s32[]{:T(128)} %get-tuple-element.72, bf16[2048,128]{1,0:T(8,128)(2,1)} %get-tuple-element.80, s32[512]{0:T(512)S(1)} %bitcast.42), kind=kOutput, calls=%fused_computation.5.clone.1 | convolution fusion | flops 269549568 | bytes 657920 | tf_op jit(solution)/shard_map/while/body/eval_jaxpr/dot_general | solution.py:77
  12.3 2.5 %fusion.47 = bf16[16,512,128]{2,1,0:T(8,128)(2,1)} fusion(bf16[16,512,128]{2,1,0:T(8,128)(2,1)} %get-tuple-element.73, s32[]{:T(128)} %get-tuple-element.72, bf16[2048,128]{1,0:T(8,128)(2,1)} %get-tuple-element.80, s32[512]{0:T(512)S(1)} %bitcast.42), kind=kOutput, calls=%fused_computation.5.clone.1 | convolution fusion | flops 269549568 | bytes 657920 | tf_op jit(solution)/shard_map/while/body/eval_jaxpr/dot_general | solution.py:77
  14.8 2.5 %fusion.47 = bf16[16,512,128]{2,1,0:T(8,128)(2,1)} fusion(bf16[16,512,128]{2,1,0:T(8,128)(2,1)} %get-tuple-element.73, s32[]{:T(128)} %get-tuple-element.72, bf16[2048,128]{1,0:T(8,128)(2,1)} %get-tuple-element.80, s32[512]{0:T(512)S(1)} %bitcast.42), kind=kOutput, calls=%fused_computation.5.clone.1 | convolution fusion | flops 269549568 | bytes 657920 | tf_op jit(solution)/shard_map/while/body/eval_jaxpr/dot_general | solution.py:77
  17.4 2.5 %fusion.47 = bf16[16,512,128]{2,1,0:T(8,128)(2,1)} fusion(bf16[16,512,128]{2,1,0:T(8,128)(2,1)} %get-tuple-element.73, s32[]{:T(128)} %get-tuple-element.72, bf16[2048,128]{1,0:T(8,128)(2,1)} %get-tuple-element.80, s32[512]{0:T(512)S(1)} %bitcast.42), kind=kOutput, calls=%fused_computation.5.clone.1 | convolution fusion | flops 269549568 | bytes 657920 | tf_op jit(solution)/shard_map/while/body/eval_jaxpr/dot_general | solution.py:77
  19.9 2.5 %fusion.47 = bf16[16,512,128]{2,1,0:T(8,128)(2,1)} fusion(bf16[16,512,128]{2,1,0:T(8,128)(2,1)} %get-tuple-element.73, s32[]{:T(128)} %get-tuple-element.72, bf16[2048,128]{1,0:T(8,128)(2,1)} %get-tuple-element.80, s32[512]{0:T(512)S(1)} %bitcast.42), kind=kOutput, calls=%fused_computation.5.clone.1 | convolution fusion | flops 269549568 | bytes 657920 | tf_op jit(solution)/shard_map/while/body/eval_jaxpr/dot_general | solution.py:77
  22.5 2.5 %fusion.47 = bf16[16,512,128]{2,1,0:T(8,128)(2,1)} fusion(bf16[16,512,128]{2,1,0:T(8,128)(2,1)} %get-tuple-element.73, s32[]{:T(128)} %get-tuple-element.72, bf16[2048,128]{1,0:T(8,128)(2,1)} %get-tuple-element.80, s32[512]{0:T(512)S(1)} %bitcast.42), kind=kOutput, calls=%fused_computation.5.clone.1 | convolution fusion | flops 269549568 | bytes 657920 | tf_op jit(solution)/shard_map/while/body/eval_jaxpr/dot_general | solution.py:77
  25.0 2.5 %fusion.47 = bf16[16,512,128]{2,1,0:T(8,128)(2,1)} fusion(bf16[16,512,128]{2,1,0:T(8,128)(2,1)} %get-tuple-element.73, s32[]{:T(128)} %get-tuple-element.72, bf16[2048,128]{1,0:T(8,128)(2,1)} %get-tuple-element.80, s32[512]{0:T(512)S(1)} %bitcast.42), kind=kOutput, calls=%fused_computation.5.clone.1 | convolution fusion | flops 269549568 | bytes 657920 | tf_op jit(solution)/shard_map/while/body/eval_jaxpr/dot_general | solution.py:77
  27.6 2.5 %fusion.47 = bf16[16,512,128]{2,1,0:T(8,128)(2,1)} fusion(bf16[16,512,128]{2,1,0:T(8,128)(2,1)} %get-tuple-element.73, s32[]{:T(128)} %get-tuple-element.72, bf16[2048,128]{1,0:T(8,128)(2,1)} %get-tuple-element.80, s32[512]{0:T(512)S(1)} %bitcast.42), kind=kOutput, calls=%fused_computation.5.clone.1 | convolution fusion | flops 269549568 | bytes 657920 | tf_op jit(solution)/shard_map/while/body/eval_jaxpr/dot_general | solution.py:77
  30.1 2.5 %fusion.47 = bf16[16,512,128]{2,1,0:T(8,128)(2,1)} fusion(bf16[16,512,128]{2,1,0:T(8,128)(2,1)} %get-tuple-element.73, s32[]{:T(128)} %get-tuple-element.72, bf16[2048,128]{1,0:T(8,128)(2,1)} %get-tuple-element.80, s32[512]{0:T(512)S(1)} %bitcast.42), kind=kOutput, calls=%fused_computation.5.clone.1 | convolution fusion | flops 269549568 | bytes 657920 | tf_op jit(solution)/shard_map/while/body/eval_jaxpr/dot_general | solution.py:77
  32.7 2.5 %fusion.47 = bf16[16,512,128]{2,1,0:T(8,128)(2,1)} fusion(bf16[16,512,128]{2,1,0:T(8,128)(2,1)} %get-tuple-element.73, s32[]{:T(128)} %get-tuple-element.72, bf16[2048,128]{1,0:T(8,128)(2,1)} %get-tuple-element.80, s32[512]{0:T(512)S(1)} %bitcast.42), kind=kOutput, calls=%fused_computation.5.clone.1 | convolution fusion | flops 269549568 | bytes 657920 | tf_op jit(solution)/shard_map/while/body/eval_jaxpr/dot_general | solution.py:77
  35.2 2.5 %fusion.47 = bf16[16,512,128]{2,1,0:T(8,128)(2,1)} fusion(bf16[16,512,128]{2,1,0:T(8,128)(2,1)} %get-tuple-element.73, s32[]{:T(128)} %get-tuple-element.72, bf16[2048,128]{1,0:T(8,128)(2,1)} %get-tuple-element.80, s32[512]{0:T(512)S(1)} %bitcast.42), kind=kOutput, calls=%fused_computation.5.clone.1 | convolution fusion | flops 269549568 | bytes 657920 | tf_op jit(solution)/shard_map/while/body/eval_jaxpr/dot_general | solution.py:77
  37.8 2.5 %fusion.47 = bf16[16,512,128]{2,1,0:T(8,128)(2,1)} fusion(bf16[16,512,128]{2,1,0:T(8,128)(2,1)} %get-tuple-element.73, s32[]{:T(128)} %get-tuple-element.72, bf16[2048,128]{1,0:T(8,128)(2,1)} %get-tuple-element.80, s32[512]{0:T(512)S(1)} %bitcast.42), kind=kOutput, calls=%fused_computation.5.clone.1 | convolution fusion | flops 269549568 | bytes 657920 | tf_op jit(solution)/shard_map/while/body/eval_jaxpr/dot_general | solution.py:77
  40.3 2.5 %fusion.47 = bf16[16,512,128]{2,1,0:T(8,128)(2,1)} fusion(bf16[16,512,128]{2,1,0:T(8,128)(2,1)} %get-tuple-element.73, s32[]{:T(128)} %get-tuple-element.72, bf16[2048,128]{1,0:T(8,128)(2,1)} %get-tuple-element.80, s32[512]{0:T(512)S(1)} %bitcast.42), kind=kOutput, calls=%fused_computation.5.clone.1 | convolution fusion | flops 269549568 | bytes 657920 | tf_op jit(solution)/shard_map/while/body/eval_jaxpr/dot_general | solution.py:77
  42.9 16.6 %all-to-all-start = ((bf16[256,1,32,128]{3,2,1,0:T(8,128)(2,1)}), bf16[256,1,32,128]{3,2,1,0:T(8,128)(2,1)}, u32[]{:S(2)}, u32[]{:S(2)}) async-start(bf16[256,1,32,128]{3,2,1,0:T(8,128)(2,1)} %bitcast.4), calls=%async_computation | async-start | bytes 4194304 | tf_op jit(solution)/shard_map/all_to_all | solution.py:28
  59.5 2.5 %copy.24 = bf16[1,1,2048,512]{2,3,1,0:T(8,128)(2,1)} copy(bf16[1,1,2048,512]{3,2,1,0:T(8,128)(2,1)S(1)} %copy-done.1) | data formatting | bytes 4194304 | tf_op args[2]
  62.0 10.9 %all_gather.3 = bf16[160,512]{1,0:T(8,128)(2,1)S(1)} all-gather(bf16[160,128]{1,0:T(8,128)(2,1)S(1)} %copy-done.5), channel_id=1, replica_groups=mesh['band'=64,'feat'=4] {'feat'}, dimensions={1}, use_global_device_ids=true | all-gather | bytes 204800 | tf_op jit(solution)/shard_map/all_gather | solution.py:112
  72.9 1.3 fusion.16
  74.2 4.2 %fusion.8 = f32[2048,512]{1,0:T(8,128)} fusion(bf16[1,1,2048,512]{3,2,1,0:T(8,128)(2,1)S(1)} %copy-done.1, bf16[1536,512]{1,0:T(8,128)(2,1)} %param.24), kind=kOutput, calls=%fused_computation.14 | convolution fusion | flops 1073741824 | bytes 6815744 | tf_op jit(solution)/shard_map/dot_general | solution.py:124
  78.5 35.0 %all-to-all-done = bf16[256,1,32,128]{3,2,1,0:T(8,128)(2,1)} async-done(((bf16[256,1,32,128]{3,2,1,0:T(8,128)(2,1)}), bf16[256,1,32,128]{3,2,1,0:T(8,128)(2,1)}, u32[]{:S(2)}, u32[]{:S(2)}) %all-to-all-start) | async-done | bytes 2097184 | tf_op jit(solution)/shard_map/all_to_all | solution.py:28
  113.5 2.7 %copy.25 = bf16[64,32,4,128]{3,2,1,0:T(4,128)(2,1)S(1)} copy(bf16[64,32,4,128]{3,1,2,0:T(8,128)(2,1)} %bitcast.8) | data formatting | bytes 4194304 | tf_op jit(solution)/shard_map/transpose | solution.py:17
  116.2 2.4 %fusion.5 = f32[2048,512]{1,0:T(8,128)S(1)} fusion(bf16[256,8,4,128]{3,2,1,0:T(4,128)(2,1)S(1)} %bitcast.41, bf16[1536,512]{1,0:T(8,128)(2,1)} %param.24), kind=kOutput, calls=%fused_computation.11 | convolution fusion | flops 1073741824 | bytes 6815744 | tf_op jit(solution)/shard_map/dot_general | solution.py:125
  118.7 3.0 %multiply_convert_fusion = bf16[2048,512]{1,0:T(8,128)(2,1)S(1)} fusion(f32[2048,512]{1,0:T(8,128)S(1)} %copy-done.2, f32[2048,512]{1,0:T(8,128)S(1)} %fusion.5, f32[160,512]{1,0:T(8,128)S(1)} %fusion.16, f32[512]{0:T(512)S(1)} %copy-done.9, s32[2048]{0:T(1024)S(1)} %broadcast_minimum_fusion), kind=kOutput, calls=%fused_computation.9 | convolution fusion | flops 2021982208 | bytes 10823680 | tf_op jit(solution)/shard_map/dot_general | solution.py:117
  121.7 1.4 add_reduce_fusion
  123.8 0.9 copy-done.3
  124.7 1.6 %fusion.12 = bf16[160,512]{1,0:T(8,128)(2,1)S(1)} fusion(f32[2048,512]{0,1:T(8,128)S(1)} %get-tuple-element.39, bf16[1,1,2048,512]{2,3,1,0:T(8,128)(2,1)S(1)} %copy-done.3, f32[512]{0:T(512)S(1)} %copy-done.10, f32[512]{0:T(512)S(1)} %copy-done.11, f32[2048]{0:T(1024)S(1)} %add_rsqrt_fusion, f32[2048]{0:T(1024)S(1)} %broadcast_multiply_fusion, ...), kind=kOutput, calls=%fused_computation.22 | convolution fusion | flops 344342528 | bytes 6486016 | tf_op jit(solution)/shard_map/dot_general | solution.py:135
  127.2 3.5 %all-to-all-start.1 = ((bf16[4,160,512]{2,1,0:T(8,128)(2,1)}), bf16[4,160,512]{2,1,0:T(8,128)(2,1)S(1)}, u32[]{:S(2)}, u32[]{:S(2)}) async-start(bf16[4,160,512]{2,1,0:T(8,128)(2,1)} %broadcast_in_dim.10), calls=%async_computation.1 | async-start | bytes 1310720 | tf_op jit(solution)/shard_map/all_to_all | solution.py:35
  132.5 8.3 %all-to-all-done.1 = bf16[4,160,512]{2,1,0:T(8,128)(2,1)S(1)} async-done(((bf16[4,160,512]{2,1,0:T(8,128)(2,1)}), bf16[4,160,512]{2,1,0:T(8,128)(2,1)S(1)}, u32[]{:S(2)}, u32[]{:S(2)}) %all-to-all-start.1) | async-done | bytes 655392 | tf_op jit(solution)/shard_map/all_to_all | solution.py:35
  (60 shorter events, 5.6 us)
Async XLA Ops:
  0.0 121.7 %copy-start = (bf16[512,512]{1,0:T(8,128)(2,1)S(1)}, bf16[512,512]{1,0:T(8,128)(2,1)}, u32[]{:S(2)}) copy-start(bf16[512,512]{1,0:T(8,128)(2,1)} %param.26) | copy-start | bytes 1572868
  42.9 16.7 %copy-start.1 = (bf16[1,1,2048,512]{3,2,1,0:T(8,128)(2,1)S(1)}, bf16[1,1,2048,512]{3,2,1,0:T(8,128)(2,1)}, u32[]{:S(2)}) copy-start(bf16[1,1,2048,512]{3,2,1,0:T(8,128)(2,1)} %param.21) | copy-start | bytes 6291460
  42.9 19.2 %copy-start.5 = (bf16[160,128]{1,0:T(8,128)(2,1)S(1)}, bf16[160,128]{1,0:T(8,128)(2,1)}, u32[]{:S(2)}) copy-start(bf16[160,128]{1,0:T(8,128)(2,1)} %param.20) | copy-start | bytes 122884
  42.9 30.1 %copy-start.6 = (s32[1,1,2048]{2,1,0:T(1,128)S(1)}, s32[1,1,2048]{2,1,0:T(1,128)}, u32[]{:S(2)}) copy-start(s32[1,1,2048]{2,1,0:T(1,128)} %param.23) | copy-start | bytes 24580
  42.9 70.6 %all-to-all-start = ((bf16[256,1,32,128]{3,2,1,0:T(8,128)(2,1)}), bf16[256,1,32,128]{3,2,1,0:T(8,128)(2,1)}, u32[]{:S(2)}, u32[]{:S(2)}) async-start(bf16[256,1,32,128]{3,2,1,0:T(8,128)(2,1)} %bitcast.4), calls=%async_computation | async-start | bytes 4194304 | tf_op jit(solution)/shard_map/all_to_all | solution.py:28
  116.2 2.5 %copy-start.2 = (f32[2048,512]{1,0:T(8,128)S(1)}, f32[2048,512]{1,0:T(8,128)}, u32[]{:S(2)}) copy-start(f32[2048,512]{1,0:T(8,128)} %fusion.8) | copy-start | bytes 12582916
  116.2 2.5 %copy-start.9 = (f32[512]{0:T(512)S(1)}, f32[512]{0:T(512)}, u32[]{:S(2)}) copy-start(f32[512]{0:T(512)} %param.25) | copy-start | bytes 6148
  118.6 3.0 %copy-start.7 = (f32[512]{0:T(512)S(1)}, f32[512]{0:T(512)}, u32[]{:S(2)}) copy-start(f32[512]{0:T(512)} %param.27) | copy-start | bytes 6148
  123.1 1.6 %copy-start.3 = (bf16[1,1,2048,512]{2,3,1,0:T(8,128)(2,1)S(1)}, bf16[1,1,2048,512]{2,3,1,0:T(8,128)(2,1)}, u32[]{:S(2)}) copy-start(bf16[1,1,2048,512]{2,3,1,0:T(8,128)(2,1)} %copy.24) | copy-start | bytes 6291460
  123.1 1.6 %copy-start.10 = (f32[512]{0:T(512)S(1)}, f32[512]{0:T(512)}, u32[]{:S(2)}) copy-start(f32[512]{0:T(512)} %param.29) | copy-start | bytes 6148
  123.1 1.6 %copy-start.11 = (f32[512]{0:T(512)S(1)}, f32[512]{0:T(512)}, u32[]{:S(2)}) copy-start(f32[512]{0:T(512)} %param.28) | copy-start | bytes 6148
  124.7 7.6 %copy-start.4 = (bf16[1024,512]{1,0:T(8,128)(2,1)S(1)}, bf16[1024,512]{1,0:T(8,128)(2,1)}, u32[]{:S(2)}) copy-start(bf16[1024,512]{1,0:T(8,128)(2,1)} %param.30) | copy-start | bytes 3145732
  124.7 16.2 %copy-start.8 = (bf16[512,512]{1,0:T(8,128)(2,1)S(1)}, bf16[512,512]{1,0:T(8,128)(2,1)}, u32[]{:S(2)}) copy-start(bf16[512,512]{1,0:T(8,128)(2,1)} %param.32) | copy-start | bytes 1572868
  124.7 16.2 %copy-start.12 = (f32[512]{0:T(512)S(1)}, f32[512]{0:T(512)}, u32[]{:S(2)}) copy-start(f32[512]{0:T(512)} %param.33) | copy-start | bytes 6148
  124.7 16.2 %copy-start.13 = (f32[512]{0:T(512)S(1)}, f32[512]{0:T(512)}, u32[]{:S(2)}) copy-start(f32[512]{0:T(512)} %param.31) | copy-start | bytes 6148
  127.2 13.5 %all-to-all-start.1 = ((bf16[4,160,512]{2,1,0:T(8,128)(2,1)}), bf16[4,160,512]{2,1,0:T(8,128)(2,1)S(1)}, u32[]{:S(2)}, u32[]{:S(2)}) async-start(bf16[4,160,512]{2,1,0:T(8,128)(2,1)} %broadcast_in_dim.10), calls=%async_computation.1 | async-start | bytes 1310720 | tf_op jit(solution)/shard_map/all_to_all | solution.py:35
where the time goes:
time: 144 us; the launch traced here: 142 us
  matrix products  55.5 us (39%)
  waiting for transfers between devices  43.3 us (30%)
  starting transfers between devices  20.1 us (14%)
  blocking collectives  10.9 us (8%)
  local copies, waits for them, and re-layouts  9.17 us (6%)
  other arithmetic  3.13 us (2%)
    dot_general x16, matrix products, one_block(): jnp.dot(onehot, table, preferred_element_type=jnp.float32)  40.7 us
    all_to_all x1, waiting for transfers between devices, joined_exchange(): tiles = lax.all_to_all(tiles, axis, split_axis=0, concat_axis=0, tiled=True)  35 us
    all_to_all x1, starting transfers between devices, joined_exchange(): tiles = lax.all_to_all(tiles, axis, split_axis=0, concat_axis=0, tiled=True)  16.6 us
    all_gather x1, blocking collectives, body(): portion = lax.all_gather(mesh_latent, 'feat', axis=1, tiled=True)  10.9 us
    all_to_all x1, waiting for transfers between devices, from_everyone(): lax.all_to_all(jnp.broadcast_to(value[None], (length, *value.shape)), axi...  8.27 us
    dot_general x1, matrix products, body(): jnp.dot(own_edges, edge_w1[:full_width], preferred_element_type=jnp.float32)  4.24 us
    unnamed x30, local copies, waits for them, and re-layouts  3.98 us
    all_to_all x1, starting transfers between devices, from_everyone(): lax.all_to_all(jnp.broadcast_to(value[None], (length, *value.shape)), axi...  3.48 us
  transfers between devices with their start and end apart: 2, of which 2 were waited for; matrix products, arithmetic and copies ran while one was open for 7% of the time, Pallas kernels for 0%

commit v1 on v0

--- a/solution.py
+++ b/solution.py
@@ -109,7 +109,9 @@
     own_edges = edge_latent.reshape(-1, full_width)
     targets = edge_dst.reshape(-1)
     recv_weight = edge_w1[2 * full_width :]
-    portion = lax.all_gather(mesh_latent, "feat", axis=1, tiled=True)
+    portion = jnp.concatenate(
+        lax.all_to_all(jnp.stack([mesh_latent] * lax.axis_size("feat")), "feat", 0, 0), axis=1
+    )
     projected = jnp.dot(portion, recv_weight, preferred_element_type=jnp.float32)
     node_ids = lax.broadcasted_iota(jnp.int32, (mesh_count, targets.shape[0]), 0)
     clipped = jnp.minimum(targets, mesh_count - 1)

time: 144 us -> 150 us (1.042)
  waiting for transfers between devices: 43.3 us -> 54.2 us
  blocking collectives: 10.9 us -> 0 us
  starting transfers between devices: 20.1 us -> 24.9 us
  local copies, waits for them, and re-layouts: 9.17 us -> 10.8 us
    all_gather x1 -> x0, blocking collectives: 10.9 us -> none  [body(): portion = lax.all_gather(mesh_latent, 'feat', axis=1, tiled=True)]
    all_to_all x1, waiting for transfers between devices: 35 us -> 45.9 us  [joined_exchange(): tiles = lax.all_to_all(tiles, axis, split_axis=0, concat_axis=0, tiled=True)]
    all_to_all x0 -> x1, starting transfers between devices: none -> 4.83 us  [body(): lax.all_to_all(jnp.stack([mesh_latent] * lax.axis_size('feat')), 'feat',...]
    another operation x0 -> x1, local copies, waits for them, and re-layouts: none -> 1.52 us  [body(): jnp.stack([mesh_latent] * lax.axis_size('feat'))]
    unnamed x30 -> x28, local copies, waits for them, and re-layouts: 3.98 us -> 4.06 us
  transfers between devices with their start and end apart: 2 -> 3, of which waited for: 2 -> 2; matrix products, arithmetic and copies ran while one was open for 7% -> 35% of each run, Pallas kernels for 0% -> 0%
where the time goes in v1:
time: 150 us; the launch traced here: 149 us
  matrix products  55.4 us (37%)
  waiting for transfers between devices  54.2 us (36%)
  starting transfers between devices  24.9 us (17%)
  local copies, waits for them, and re-layouts  10.8 us (7%)
  other arithmetic  3.14 us (2%)
    all_to_all x1, waiting for transfers between devices, joined_exchange(): tiles = lax.all_to_all(tiles, axis, split_axis=0, concat_axis=0, tiled=True)  45.9 us
    dot_general x16, matrix products, one_block(): jnp.dot(onehot, table, preferred_element_type=jnp.float32)  40.6 us
    all_to_all x1, starting transfers between devices, joined_exchange(): tiles = lax.all_to_all(tiles, axis, split_axis=0, concat_axis=0, tiled=True)  16.6 us
    all_to_all x1, waiting for transfers between devices, from_everyone(): lax.all_to_all(jnp.broadcast_to(value[None], (length, *value.shape)), axi...  8.25 us
    all_to_all x1, starting transfers between devices, body(): lax.all_to_all(jnp.stack([mesh_latent] * lax.axis_size('feat')), 'feat',...  4.83 us
    dot_general x1, matrix products, body(): jnp.dot(own_edges, edge_w1[:full_width], preferred_element_type=jnp.float32)  4.22 us
    unnamed x28, local copies, waits for them, and re-layouts  4.06 us
    all_to_all x1, starting transfers between devices, from_everyone(): lax.all_to_all(jnp.broadcast_to(value[None], (length, *value.shape)), axi...  3.48 us
  transfers between devices with their start and end apart: 3, of which 2 were waited for; matrix products, arithmetic and copies ran while one was open for 35% of the time, Pallas kernels for 0%

profile of v1, /device:TPU:1, one launch (start us, length us, event | category | flops | bytes accessed | tf_op | source)
XLA Modules:
  0.0 148.7 jit_solution(6651351737301126384)
XLA Ops:
  0.0 1.5 %stack.2 = bf16[4,160,128]{2,1,0:T(8,128)(2,1)} broadcast(bf16[160,128]{1,0:T(8,128)(2,1)} %param.20), dimensions={1,2} | broadcast | bytes 204800 | tf_op jit(solution)/shard_map/stack | solution.py:113
  1.5 4.8 %all-to-all-start = ((bf16[4,160,128]{2,1,0:T(8,128)(2,1)}), bf16[4,160,128]{2,1,0:T(8,128)(2,1)S(1)}, u32[]{:S(2)}, u32[]{:S(2)}) async-start(bf16[4,160,128]{2,1,0:T(8,128)(2,1)} %stack.2), calls=%async_computation | async-start | bytes 327680 | tf_op jit(solution)/shard_map/all_to_all | solution.py:113
  6.9 1.5 reduce.4
  8.4 40.8 %while.10 = (s32[]{:T(128)}, bf16[16,512,128]{2,1,0:T(8,128)(2,1)}, s32[16,512]{1,0:T(8,128)S(1)}, bf16[2048,128]{1,0:T(8,128)(2,1)}, s32[]{:T(128)}) while((s32[]{:T(128)}, bf16[16,512,128]{2,1,0:T(8,128)(2,1)}, s32[16,512]{1,0:T(8,128)S(1)}, bf16[2048,128]{1,0:T(8,128)(2,1)}, s32[]{:T(128)}) %tuple.21), condition=%wide.region_1.2_spmd, body=%wide.region_0.1_spmd.sunk | while | flops 269549568 | bytes 662081 | solution.py:79
  8.4 2.5 %fusion.48 = bf16[16,512,128]{2,1,0:T(8,128)(2,1)} fusion(bf16[16,512,128]{2,1,0:T(8,128)(2,1)} %get-tuple-element.73, s32[]{:T(128)} %get-tuple-element.72, bf16[2048,128]{1,0:T(8,128)(2,1)} %get-tuple-element.80, s32[512]{0:T(512)S(1)} %bitcast.54), kind=kOutput, calls=%fused_computation.5.clone.1 | convolution fusion | flops 269549568 | bytes 657920 | tf_op jit(solution)/shard_map/while/body/eval_jaxpr/dot_general | solution.py:77
  11.0 2.5 %fusion.48 = bf16[16,512,128]{2,1,0:T(8,128)(2,1)} fusion(bf16[16,512,128]{2,1,0:T(8,128)(2,1)} %get-tuple-element.73, s32[]{:T(128)} %get-tuple-element.72, bf16[2048,128]{1,0:T(8,128)(2,1)} %get-tuple-element.80, s32[512]{0:T(512)S(1)} %bitcast.54), kind=kOutput, calls=%fused_computation.5.clone.1 | convolution fusion | flops 269549568 | bytes 657920 | tf_op jit(solution)/shard_map/while/body/eval_jaxpr/dot_general | solution.py:77
  13.5 2.5 %fusion.48 = bf16[16,512,128]{2,1,0:T(8,128)(2,1)} fusion(bf16[16,512,128]{2,1,0:T(8,128)(2,1)} %get-tuple-element.73, s32[]{:T(128)} %get-tuple-element.72, bf16[2048,128]{1,0:T(8,128)(2,1)} %get-tuple-element.80, s32[512]{0:T(512)S(1)} %bitcast.54), kind=kOutput, calls=%fused_computation.5.clone.1 | convolution fusion | flops 269549568 | bytes 657920 | tf_op jit(solution)/shard_map/while/body/eval_jaxpr/dot_general | solution.py:77
  16.1 2.5 %fusion.48 = bf16[16,512,128]{2,1,0:T(8,128)(2,1)} fusion(bf16[16,512,128]{2,1,0:T(8,128)(2,1)} %get-tuple-element.73, s32[]{:T(128)} %get-tuple-element.72, bf16[2048,128]{1,0:T(8,128)(2,1)} %get-tuple-element.80, s32[512]{0:T(512)S(1)} %bitcast.54), kind=kOutput, calls=%fused_computation.5.clone.1 | convolution fusion | flops 269549568 | bytes 657920 | tf_op jit(solution)/shard_map/while/body/eval_jaxpr/dot_general | solution.py:77
  18.6 2.5 %fusion.48 = bf16[16,512,128]{2,1,0:T(8,128)(2,1)} fusion(bf16[16,512,128]{2,1,0:T(8,128)(2,1)} %get-tuple-element.73, s32[]{:T(128)} %get-tuple-element.72, bf16[2048,128]{1,0:T(8,128)(2,1)} %get-tuple-element.80, s32[512]{0:T(512)S(1)} %bitcast.54), kind=kOutput, calls=%fused_computation.5.clone.1 | convolution fusion | flops 269549568 | bytes 657920 | tf_op jit(solution)/shard_map/while/body/eval_jaxpr/dot_general | solution.py:77
  21.2 2.5 %fusion.48 = bf16[16,512,128]{2,1,0:T(8,128)(2,1)} fusion(bf16[16,512,128]{2,1,0:T(8,128)(2,1)} %get-tuple-element.73, s32[]{:T(128)} %get-tuple-element.72, bf16[2048,128]{1,0:T(8,128)(2,1)} %get-tuple-element.80, s32[512]{0:T(512)S(1)} %bitcast.54), kind=kOutput, calls=%fused_computation.5.clone.1 | convolution fusion | flops 269549568 | bytes 657920 | tf_op jit(solution)/shard_map/while/body/eval_jaxpr/dot_general | solution.py:77
  23.7 2.5 %fusion.48 = bf16[16,512,128]{2,1,0:T(8,128)(2,1)} fusion(bf16[16,512,128]{2,1,0:T(8,128)(2,1)} %get-tuple-element.73, s32[]{:T(128)} %get-tuple-element.72, bf16[2048,128]{1,0:T(8,128)(2,1)} %get-tuple-element.80, s32[512]{0:T(512)S(1)} %bitcast.54), kind=kOutput, calls=%fused_computation.5.clone.1 | convolution fusion | flops 269549568 | bytes 657920 | tf_op jit(solution)/shard_map/while/body/eval_jaxpr/dot_general | solution.py:77
  26.3 2.5 %fusion.48 = bf16[16,512,128]{2,1,0:T(8,128)(2,1)} fusion(bf16[16,512,128]{2,1,0:T(8,128)(2,1)} %get-tuple-element.73, s32[]{:T(128)} %get-tuple-element.72, bf16[2048,128]{1,0:T(8,128)(2,1)} %get-tuple-element.80, s32[512]{0:T(512)S(1)} %bitcast.54), kind=kOutput, calls=%fused_computation.5.clone.1 | convolution fusion | flops 269549568 | bytes 657920 | tf_op jit(solution)/shard_map/while/body/eval_jaxpr/dot_general | solution.py:77
  28.8 2.5 %fusion.48 = bf16[16,512,128]{2,1,0:T(8,128)(2,1)} fusion(bf16[16,512,128]{2,1,0:T(8,128)(2,1)} %get-tuple-element.73, s32[]{:T(128)} %get-tuple-element.72, bf16[2048,128]{1,0:T(8,128)(2,1)} %get-tuple-element.80, s32[512]{0:T(512)S(1)} %bitcast.54), kind=kOutput, calls=%fused_computation.5.clone.1 | convolution fusion | flops 269549568 | bytes 657920 | tf_op jit(solution)/shard_map/while/body/eval_jaxpr/dot_general | solution.py:77
  31.4 2.5 %fusion.48 = bf16[16,512,128]{2,1,0:T(8,128)(2,1)} fusion(bf16[16,512,128]{2,1,0:T(8,128)(2,1)} %get-tuple-element.73, s32[]{:T(128)} %get-tuple-element.72, bf16[2048,128]{1,0:T(8,128)(2,1)} %get-tuple-element.80, s32[512]{0:T(512)S(1)} %bitcast.54), kind=kOutput, calls=%fused_computation.5.clone.1 | convolution fusion | flops 269549568 | bytes 657920 | tf_op jit(solution)/shard_map/while/body/eval_jaxpr/dot_general | solution.py:77
  33.9 2.5 %fusion.48 = bf16[16,512,128]{2,1,0:T(8,128)(2,1)} fusion(bf16[16,512,128]{2,1,0:T(8,128)(2,1)} %get-tuple-element.73, s32[]{:T(128)} %get-tuple-element.72, bf16[2048,128]{1,0:T(8,128)(2,1)} %get-tuple-element.80, s32[512]{0:T(512)S(1)} %bitcast.54), kind=kOutput, calls=%fused_computation.5.clone.1 | convolution fusion | flops 269549568 | bytes 657920 | tf_op jit(solution)/shard_map/while/body/eval_jaxpr/dot_general | solution.py:77
  36.5 2.5 %fusion.48 = bf16[16,512,128]{2,1,0:T(8,128)(2,1)} fusion(bf16[16,512,128]{2,1,0:T(8,128)(2,1)} %get-tuple-element.73, s32[]{:T(128)} %get-tuple-element.72, bf16[2048,128]{1,0:T(8,128)(2,1)} %get-tuple-element.80, s32[512]{0:T(512)S(1)} %bitcast.54), kind=kOutput, calls=%fused_computation.5.clone.1 | convolution fusion | flops 269549568 | bytes 657920 | tf_op jit(solution)/shard_map/while/body/eval_jaxpr/dot_general | solution.py:77
  39.0 2.5 %fusion.48 = bf16[16,512,128]{2,1,0:T(8,128)(2,1)} fusion(bf16[16,512,128]{2,1,0:T(8,128)(2,1)} %get-tuple-element.73, s32[]{:T(128)} %get-tuple-element.72, bf16[2048,128]{1,0:T(8,128)(2,1)} %get-tuple-element.80, s32[512]{0:T(512)S(1)} %bitcast.54), kind=kOutput, calls=%fused_computation.5.clone.1 | convolution fusion | flops 269549568 | bytes 657920 | tf_op jit(solution)/shard_map/while/body/eval_jaxpr/dot_general | solution.py:77
  41.6 2.5 %fusion.48 = bf16[16,512,128]{2,1,0:T(8,128)(2,1)} fusion(bf16[16,512,128]{2,1,0:T(8,128)(2,1)} %get-tuple-element.73, s32[]{:T(128)} %get-tuple-element.72, bf16[2048,128]{1,0:T(8,128)(2,1)} %get-tuple-element.80, s32[512]{0:T(512)S(1)} %bitcast.54), kind=kOutput, calls=%fused_computation.5.clone.1 | convolution fusion | flops 269549568 | bytes 657920 | tf_op jit(solution)/shard_map/while/body/eval_jaxpr/dot_general | solution.py:77
  44.1 2.5 %fusion.48 = bf16[16,512,128]{2,1,0:T(8,128)(2,1)} fusion(bf16[16,512,128]{2,1,0:T(8,128)(2,1)} %get-tuple-element.73, s32[]{:T(128)} %get-tuple-element.72, bf16[2048,128]{1,0:T(8,128)(2,1)} %get-tuple-element.80, s32[512]{0:T(512)S(1)} %bitcast.54), kind=kOutput, calls=%fused_computation.5.clone.1 | convolution fusion | flops 269549568 | bytes 657920 | tf_op jit(solution)/shard_map/while/body/eval_jaxpr/dot_general | solution.py:77
  46.6 2.5 %fusion.48 = bf16[16,512,128]{2,1,0:T(8,128)(2,1)} fusion(bf16[16,512,128]{2,1,0:T(8,128)(2,1)} %get-tuple-element.73, s32[]{:T(128)} %get-tuple-element.72, bf16[2048,128]{1,0:T(8,128)(2,1)} %get-tuple-element.80, s32[512]{0:T(512)S(1)} %bitcast.54), kind=kOutput, calls=%fused_computation.5.clone.1 | convolution fusion | flops 269549568 | bytes 657920 | tf_op jit(solution)/shard_map/while/body/eval_jaxpr/dot_general | solution.py:77
  49.2 16.6 %all-to-all-start.1 = ((bf16[256,1,32,128]{3,2,1,0:T(8,128)(2,1)}), bf16[256,1,32,128]{3,2,1,0:T(8,128)(2,1)}, u32[]{:S(2)}, u32[]{:S(2)}) async-start(bf16[256,1,32,128]{3,2,1,0:T(8,128)(2,1)} %bitcast.5), calls=%async_computation.1 | async-start | bytes 4194304 | tf_op jit(solution)/shard_map/all_to_all | solution.py:28
  65.8 2.5 %copy.26 = bf16[1,1,2048,512]{2,3,1,0:T(8,128)(2,1)} copy(bf16[1,1,2048,512]{3,2,1,0:T(8,128)(2,1)S(1)} %copy-done.1) | data formatting | bytes 4194304 | tf_op args[2]
  68.4 4.2 %fusion.8 = f32[2048,512]{1,0:T(8,128)} fusion(bf16[1,1,2048,512]{3,2,1,0:T(8,128)(2,1)S(1)} %copy-done.1, bf16[1536,512]{1,0:T(8,128)(2,1)} %param.24), kind=kOutput, calls=%fused_computation.14 | convolution fusion | flops 1073741824 | bytes 6815744 | tf_op jit(solution)/shard_map/dot_general | solution.py:126
  72.6 1.3 fusion.16
  73.9 45.9 %all-to-all-done.1 = bf16[256,1,32,128]{3,2,1,0:T(8,128)(2,1)} async-done(((bf16[256,1,32,128]{3,2,1,0:T(8,128)(2,1)}), bf16[256,1,32,128]{3,2,1,0:T(8,128)(2,1)}, u32[]{:S(2)}, u32[]{:S(2)}) %all-to-all-start.1) | async-done | bytes 2097184 | tf_op jit(solution)/shard_map/all_to_all | solution.py:28
  119.8 2.7 %copy.27 = bf16[64,32,4,128]{3,2,1,0:T(4,128)(2,1)S(1)} copy(bf16[64,32,4,128]{3,1,2,0:T(8,128)(2,1)} %bitcast.9) | data formatting | bytes 4194304 | tf_op jit(solution)/shard_map/transpose | solution.py:17
  122.5 2.4 %fusion.5 = f32[2048,512]{1,0:T(8,128)S(1)} fusion(bf16[256,8,4,128]{3,2,1,0:T(4,128)(2,1)S(1)} %bitcast.53, bf16[1536,512]{1,0:T(8,128)(2,1)} %param.24), kind=kOutput, calls=%fused_computation.11 | convolution fusion | flops 1073741824 | bytes 6815744 | tf_op jit(solution)/shard_map/dot_general | solution.py:127
  125.0 3.0 %multiply_convert_fusion = bf16[2048,512]{1,0:T(8,128)(2,1)S(1)} fusion(f32[2048,512]{1,0:T(8,128)S(1)} %copy-done.2, f32[2048,512]{1,0:T(8,128)S(1)} %fusion.5, f32[160,512]{1,0:T(8,128)S(1)} %fusion.16, f32[512]{0:T(512)S(1)} %copy-done.8, s32[2048]{0:T(1024)S(1)} %broadcast_minimum_fusion), kind=kOutput, calls=%fused_computation.9 | convolution fusion | flops 2021982208 | bytes 10823680 | tf_op jit(solution)/shard_map/dot_general | solution.py:119
  128.0 1.4 add_reduce_fusion
  131.0 1.6 %fusion.12 = bf16[160,512]{1,0:T(8,128)(2,1)S(1)} fusion(f32[2048,512]{0,1:T(8,128)S(1)} %get-tuple-element.39, bf16[1,1,2048,512]{2,3,1,0:T(8,128)(2,1)S(1)} %copy-done.3, f32[512]{0:T(512)S(1)} %copy-done.9, f32[512]{0:T(512)S(1)} %copy-done.10, f32[2048]{0:T(1024)S(1)} %add_rsqrt_fusion, f32[2048]{0:T(1024)S(1)} %broadcast_multiply_fusion, ...), kind=kOutput, calls=%fused_computation.22 | convolution fusion | flops 344342528 | bytes 6486016 | tf_op jit(solution)/shard_map/dot_general | solution.py:137
  133.5 3.5 %all-to-all-start.2 = ((bf16[4,160,512]{2,1,0:T(8,128)(2,1)}), bf16[4,160,512]{2,1,0:T(8,128)(2,1)S(1)}, u32[]{:S(2)}, u32[]{:S(2)}) async-start(bf16[4,160,512]{2,1,0:T(8,128)(2,1)} %broadcast_in_dim.10), calls=%async_computation.2 | async-start | bytes 1310720 | tf_op jit(solution)/shard_map/all_to_all | solution.py:35
  138.8 8.2 %all-to-all-done.2 = bf16[4,160,512]{2,1,0:T(8,128)(2,1)S(1)} async-done(((bf16[4,160,512]{2,1,0:T(8,128)(2,1)}), bf16[4,160,512]{2,1,0:T(8,128)(2,1)S(1)}, u32[]{:S(2)}, u32[]{:S(2)}) %all-to-all-start.2) | async-done | bytes 655392 | tf_op jit(solution)/shard_map/all_to_all | solution.py:35
  (61 shorter events, 6.6 us)
Async XLA Ops:
  0.0 128.0 %copy-start = (bf16[512,512]{1,0:T(8,128)(2,1)S(1)}, bf16[512,512]{1,0:T(8,128)(2,1)}, u32[]{:S(2)}) copy-start(bf16[512,512]{1,0:T(8,128)(2,1)} %param.26) | copy-start | bytes 1572868
  1.5 47.7 %all-to-all-start = ((bf16[4,160,128]{2,1,0:T(8,128)(2,1)}), bf16[4,160,128]{2,1,0:T(8,128)(2,1)S(1)}, u32[]{:S(2)}, u32[]{:S(2)}) async-start(bf16[4,160,128]{2,1,0:T(8,128)(2,1)} %stack.2), calls=%async_computation | async-start | bytes 327680 | tf_op jit(solution)/shard_map/all_to_all | solution.py:113
  49.2 16.7 %copy-start.1 = (bf16[1,1,2048,512]{3,2,1,0:T(8,128)(2,1)S(1)}, bf16[1,1,2048,512]{3,2,1,0:T(8,128)(2,1)}, u32[]{:S(2)}) copy-start(bf16[1,1,2048,512]{3,2,1,0:T(8,128)(2,1)} %param.21) | copy-start | bytes 6291460
  49.2 19.2 %copy-start.5 = (s32[1,1,2048]{2,1,0:T(1,128)S(1)}, s32[1,1,2048]{2,1,0:T(1,128)}, u32[]{:S(2)}) copy-start(s32[1,1,2048]{2,1,0:T(1,128)} %param.23) | copy-start | bytes 24580
  49.2 70.6 %all-to-all-start.1 = ((bf16[256,1,32,128]{3,2,1,0:T(8,128)(2,1)}), bf16[256,1,32,128]{3,2,1,0:T(8,128)(2,1)}, u32[]{:S(2)}, u32[]{:S(2)}) async-start(bf16[256,1,32,128]{3,2,1,0:T(8,128)(2,1)} %bitcast.5), calls=%async_computation.1 | async-start | bytes 4194304 | tf_op jit(solution)/shard_map/all_to_all | solution.py:28
  122.5 2.5 %copy-start.2 = (f32[2048,512]{1,0:T(8,128)S(1)}, f32[2048,512]{1,0:T(8,128)}, u32[]{:S(2)}) copy-start(f32[2048,512]{1,0:T(8,128)} %fusion.8) | copy-start | bytes 12582916
  122.5 2.5 %copy-start.8 = (f32[512]{0:T(512)S(1)}, f32[512]{0:T(512)}, u32[]{:S(2)}) copy-start(f32[512]{0:T(512)} %param.25) | copy-start | bytes 6148
  124.9 3.1 %copy-start.6 = (f32[512]{0:T(512)S(1)}, f32[512]{0:T(512)}, u32[]{:S(2)}) copy-start(f32[512]{0:T(512)} %param.27) | copy-start | bytes 6148
  129.4 1.6 %copy-start.3 = (bf16[1,1,2048,512]{2,3,1,0:T(8,128)(2,1)S(1)}, bf16[1,1,2048,512]{2,3,1,0:T(8,128)(2,1)}, u32[]{:S(2)}) copy-start(bf16[1,1,2048,512]{2,3,1,0:T(8,128)(2,1)} %copy.26) | copy-start | bytes 6291460
  129.4 1.6 %copy-start.9 = (f32[512]{0:T(512)S(1)}, f32[512]{0:T(512)}, u32[]{:S(2)}) copy-start(f32[512]{0:T(512)} %param.29) | copy-start | bytes 6148
  129.4 1.6 %copy-start.10 = (f32[512]{0:T(512)S(1)}, f32[512]{0:T(512)}, u32[]{:S(2)}) copy-start(f32[512]{0:T(512)} %param.28) | copy-start | bytes 6148
  131.0 7.6 %copy-start.4 = (bf16[1024,512]{1,0:T(8,128)(2,1)S(1)}, bf16[1024,512]{1,0:T(8,128)(2,1)}, u32[]{:S(2)}) copy-start(bf16[1024,512]{1,0:T(8,128)(2,1)} %param.30) | copy-start | bytes 3145732
  132.6 14.6 %copy-start.7 = (bf16[512,512]{1,0:T(8,128)(2,1)S(1)}, bf16[512,512]{1,0:T(8,128)(2,1)}, u32[]{:S(2)}) copy-start(bf16[512,512]{1,0:T(8,128)(2,1)} %param.32) | copy-start | bytes 1572868
  132.6 14.6 %copy-start.11 = (f32[512]{0:T(512)S(1)}, f32[512]{0:T(512)}, u32[]{:S(2)}) copy-start(f32[512]{0:T(512)} %param.33) | copy-start | bytes 6148
  132.6 14.6 %copy-start.12 = (f32[512]{0:T(512)S(1)}, f32[512]{0:T(512)}, u32[]{:S(2)}) copy-start(f32[512]{0:T(512)} %param.31) | copy-start | bytes 6148
  133.5 13.5 %all-to-all-start.2 = ((bf16[4,160,512]{2,1,0:T(8,128)(2,1)}), bf16[4,160,512]{2,1,0:T(8,128)(2,1)S(1)}, u32[]{:S(2)}, u32[]{:S(2)}) async-start(bf16[4,160,512]{2,1,0:T(8,128)(2,1)} %broadcast_in_dim.10), calls=%async_computation.2 | async-start | bytes 1310720 | tf_op jit(solution)/shard_map/all_to_all | solution.py:35
